TPU v7x, 512 devices: a whole 4x4x16 slice. The times are simulated.
512 devices in a mesh: seq: 64 (over z, x), head: 8 (over y, core).
Axes of the slice: x: 4, y: 4, z: 16, core: 2. Of those that a mesh axis runs over, the one named last changes fastest.
Arguments:
- x_proj: bfloat16 [16384, 8192], P(('seq', 'head')), may hold values from -6 to 6
- z_proj: bfloat16 [16384, 8192], P(('seq', 'head')), may hold values from -6 to 6
- b_proj: bfloat16 [16384, 1024], P(('seq', 'head')), may hold values from -6 to 6
- c_proj: bfloat16 [16384, 1024], P(('seq', 'head')), may hold values from -6 to 6
- dt_raw: bfloat16 [16384, 128], P(('seq', 'head')), may hold values from -3.2 to 3.2, as said below
- dt_bias: float32 [128], P('head'), may hold values from -6.3 to -1.2, as said below
- a_log: float32 [128], P('head'), as said below
- d_skip: float32 [128], P('head'), may hold values from 0.5 to 2
- conv_x: float32 [4, 8192], P(None, 'head'), may hold values from -3 to 3
- conv_bias_x: float32 [8192], P('head'), may hold values from -3 to 3
- conv_bc: float32 [4, 2, 1024], P(None, None, 'head'), may hold values from -3 to 3
- conv_bias_bc: float32 [2, 1024], P(None, 'head'), may hold values from -3 to 3
- norm_weight: float32 [8192], P('head'), may hold values from 0.25 to 1.75
- out_weight: bfloat16 [8192, 4096], P('head', 'seq'), may hold values from -0.0625 to 0.0625
Outputs:
- mixed: bfloat16 [16384, 4096], P(('seq', 'head'))
Inputs may be any that keep to these rules, and one draw needn't show every extreme that they name: `dt_raw`: A normal draw times 0.7 plus an offset common to each head and each aligned run of 256 tokens. `dt_bias`: the inverse softplus of a per-head step size between 0.002 and 0.25. Finite; exp(a_log) lies above 0.0 and at most 0.3.
All inputs are finite; a program needn't handle non-finite values.
Results may differ from a plain program's by a relative error of at most 0.014.
Values may be sent and summed in bfloat16 or wider, within the bound.
No kernel may reach another device: no remote copies, remote signals or barrier semaphores. Data moves between devices by JAX's collectives and lax.ppermute only.
A program may use at most 128 MiB of HBM per device.

v0:
```python
import jax
import jax.numpy as jnp
from jax import lax
from jax.sharding import Mesh
from jax.sharding import PartitionSpec as P

HEAD_DIM = 64
STATE = 128
GROUPS = 8
SPAN = 128
DI = 8192
SEQ = ("seq_0", "seq_1")
SEQ_HEAD = ("seq_0", "seq_1", "head")


def from_behind(array, axis, by):
    count = lax.axis_size(axis)
    pairs = [(i, i + by) for i in range(count) if 0 <= i + by < count]
    return lax.ppermute(array, axis, pairs)


def filled_with(array, identity):
    return jax.tree.map(
        lambda a, e: jnp.broadcast_to(jnp.asarray(e, a.dtype), a.shape), array, identity
    )


def entering(array, axes, combine, identity):
    before = start = filled_with(array, identity)
    total = array
    for axis in reversed(axes):
        count, mine = (lax.axis_size(axis), lax.axis_index(axis))
        pieces = jax.tree.map(lambda part: lax.all_gather(part, axis), total)
        inside, total = (start, start)
        for k in range(count):
            passed = k < mine
            total = combine(total, jax.tree.map(lambda part: part[k], pieces))
            inside = jax.tree.map(lambda new, old: jnp.where(passed, new, old), total, inside)
        before = combine(inside, before)
    return before


def split_up(array, dim, count):
    shape = array.shape
    pieces = array.reshape(*shape[:dim], count, shape[dim] // count, *shape[dim + 1 :])
    return jnp.moveaxis(pieces, dim, 0)


def sent_and_summed(array, axis, dim):
    count = lax.axis_size(axis)
    pieces = lax.all_to_all(split_up(array, dim, count), axis, 0, 0, tiled=True)
    return jnp.sum(pieces.astype(jnp.float32), axis=0)


def depthwise(current, previous, weight, bias_row):
    padded = jnp.concatenate([previous, current], axis=0).astype(jnp.float32)
    token_count = current.shape[0]
    summed = jnp.broadcast_to(bias_row, current.shape)
    for offset in range(weight.shape[0]):
        summed = summed + weight[offset] * padded[offset : offset + token_count]
    return jax.nn.silu(summed).astype(jnp.bfloat16)


def block_weights(c_blocks, b_blocks, cumulative, step_size, per_group):
    scores = jnp.einsum("ktgn,ksgn->kgts", c_blocks, b_blocks, preferred_element_type=jnp.float32)
    by_head = jnp.transpose(cumulative, (0, 2, 1))
    spread = by_head[:, :, :, None] - by_head[:, :, None, :]
    length = cumulative.shape[1]
    causal = jnp.arange(length)[:, None] >= jnp.arange(length)[None, :]
    decays = jnp.exp(jnp.where(causal, spread, -jnp.inf))
    scaled = decays * jnp.transpose(step_size, (0, 2, 1))[:, :, None, :]
    block_count = cumulative.shape[0]
    head_count = cumulative.shape[2]
    grouped = scaled.reshape(block_count, -1, per_group, length, length) * scores[:, :, None]
    return grouped.reshape(block_count, head_count, length, length).astype(jnp.bfloat16)


def combine_states(earlier, later):
    return (earlier[0] + later[0], jnp.exp(later[0])[:, None, None] * earlier[1] + later[1])


def per_device(
    x_proj,
    z_proj,
    b_proj,
    c_proj,
    dt_raw,
    dt_bias,
    a_log,
    d_skip,
    conv_x,
    conv_bias_x,
    conv_bc,
    conv_bias_bc,
    norm_weight,
    out_weight,
):
    x_heads, z_heads, b_heads, c_heads, dt_heads = (
        lax.all_to_all(x_proj, "head", split_axis=1, concat_axis=0, tiled=True),
        lax.all_to_all(z_proj, "head", split_axis=1, concat_axis=0, tiled=True),
        lax.all_to_all(b_proj, "head", split_axis=1, concat_axis=0, tiled=True),
        lax.all_to_all(c_proj, "head", split_axis=1, concat_axis=0, tiled=True),
        lax.all_to_all(dt_raw, "head", split_axis=1, concat_axis=0, tiled=True),
    )
    kernel_len = conv_x.shape[0]
    x_cols = x_heads.shape[1]
    bc_cols = b_heads.shape[1]
    last_rows = jnp.concatenate(
        [x_heads[-(kernel_len - 1) :], b_heads[-(kernel_len - 1) :], c_heads[-(kernel_len - 1) :]],
        axis=1,
    )
    before = from_behind(last_rows, SEQ, 1)
    x_conv = depthwise(x_heads, before[:, :x_cols], conv_x, conv_bias_x)
    b_conv = depthwise(
        b_heads, before[:, x_cols : x_cols + bc_cols], conv_bc[:, 0], conv_bias_bc[0]
    )
    c_conv = depthwise(c_heads, before[:, x_cols + bc_cols :], conv_bc[:, 1], conv_bias_bc[1])
    token_count = x_conv.shape[0]
    local_heads = dt_bias.shape[0]
    local_groups = bc_cols // STATE
    per_group = local_heads // local_groups
    blocks = token_count // SPAN
    x_blocks = x_conv.reshape(blocks, SPAN, local_heads, HEAD_DIM)
    b_blocks = b_conv.reshape(blocks, SPAN, local_groups, STATE)
    c_blocks = c_conv.reshape(blocks, SPAN, local_groups, STATE)
    step_size = jax.nn.softplus(dt_heads.astype(jnp.float32) + dt_bias).reshape(
        blocks, SPAN, local_heads
    )
    cumulative = jnp.cumsum(-jnp.exp(a_log) * step_size, axis=1)
    mix_weights = block_weights(c_blocks, b_blocks, cumulative, step_size, per_group)
    y_local = jnp.einsum(
        "khts,kshp->kthp", mix_weights, x_blocks, preferred_element_type=jnp.float32
    )
    state_scale = step_size * jnp.exp(cumulative[:, -1:, :] - cumulative)
    x_weighted = (x_blocks.astype(jnp.float32) * state_scale[:, :, :, None]).astype(jnp.bfloat16)
    x_grouped = x_weighted.reshape(blocks, SPAN, local_groups, per_group, HEAD_DIM)
    pieces = jnp.einsum(
        "ksgqp,ksgn->kgqpn", x_grouped, b_blocks, preferred_element_type=jnp.float32
    )
    pieces = pieces.reshape(blocks, local_heads, HEAD_DIM, STATE)
    totals = cumulative[:, -1, :]
    final_state = jnp.zeros((local_heads, HEAD_DIM, STATE), jnp.float32)
    for block_idx in range(blocks):
        final_state = jnp.exp(totals[block_idx])[:, None, None] * final_state + pieces[block_idx]
    log_total = jnp.sum(totals, axis=0)
    carried = entering(
        (log_total, final_state),
        SEQ,
        combine_states,
        (jnp.zeros_like(log_total), jnp.zeros_like(final_state)),
    )
    running = carried[1]
    start_list = []
    for block_idx in range(blocks):
        start_list.append(running.astype(jnp.bfloat16))
        running = jnp.exp(totals[block_idx])[:, None, None] * running + pieces[block_idx]
    start_states = jnp.stack(start_list).reshape(blocks, local_groups, per_group, HEAD_DIM, STATE)
    y_carry = jnp.einsum(
        "ktgn,kgqpn->ktgqp", c_blocks, start_states, preferred_element_type=jnp.float32
    )
    y_carry = (
        y_carry.reshape(blocks, SPAN, local_heads, HEAD_DIM) * jnp.exp(cumulative)[:, :, :, None]
    )
    outputs = y_local + y_carry + d_skip[:, None] * x_blocks.astype(jnp.float32)
    outputs = outputs.reshape(token_count, local_heads * HEAD_DIM)
    gated = outputs * jax.nn.silu(z_heads.astype(jnp.float32))
    grouped = gated.reshape(token_count, -1, DI // GROUPS)
    normed = grouped / jnp.sqrt(jnp.mean(grouped * grouped, axis=-1, keepdims=True) + 1.0)
    normed = (normed.reshape(token_count, -1) * norm_weight).astype(jnp.bfloat16)
    terms = jnp.dot(
        normed,
        lax.all_gather(out_weight, SEQ, axis=1, tiled=True),
        preferred_element_type=jnp.float32,
    )
    mixed = sent_and_summed(terms.astype(jnp.bfloat16), "head", 0)
    return mixed.astype(jnp.bfloat16)


def solution(mesh):
    split = Mesh(mesh.devices.reshape(16, 4, mesh.shape["head"]), ("seq_0", "seq_1", "head"))
    return jax.shard_map(
        per_device,
        mesh=split,
        in_specs=(
            P(SEQ_HEAD, None),
            P(SEQ_HEAD, None),
            P(SEQ_HEAD, None),
            P(SEQ_HEAD, None),
            P(SEQ_HEAD, None),
            P("head"),
            P("head"),
            P("head"),
            P(None, "head"),
            P("head"),
            P(None, None, "head"),
            P(None, "head"),
            P("head"),
            P("head", SEQ),
        ),
        out_specs=P(SEQ_HEAD, None),
        check_vma=False,
    )
```

profile of v0, /device:TPU:1, one launch (start us, length us, event | category | flops | bytes accessed | tf_op | source)
XLA Modules:
  0.0 415.9 jit_solution(11446474946781498572)
XLA Ops:
  8.1 10.0 %all-to-all-start.3 = ((bf16[8,2,256]{2,1,0:T(2,128)(2,1)}), bf16[8,2,256]{2,1,0:T(2,128)(2,1)S(1)}, u32[]{:S(2)}, u32[]{:S(2)}) async-start(bf16[8,2,256]{2,1,0:T(2,128)(2,1)} %reshape.437), calls=%async_computation.3 | async-start | bytes 16384 | tf_op jit(solution)/shard_map/all_to_all | solution.py:103
  24.4 1.9 copy.87
  26.3 4.8 %all-to-all-start.1 = ((bf16[32,8,128]{2,0,1:T(8,128)(2,1)}), bf16[32,8,128]{2,0,1:T(8,128)(2,1)S(1)}, u32[]{:S(2)}, u32[]{:S(2)}) async-start(bf16[32,8,128]{2,0,1:T(8,128)(2,1)} %copy_bitcast_fusion.3), calls=%async_computation.1 | async-start | bytes 131072 | tf_op jit(solution)/shard_map/all_to_all | solution.py:101
  32.3 3.7 all-to-all-done.1
  36.0 4.0 all-to-all-start.2
  40.0 4.8 %all-to-all-done.2 = bf16[32,8,128]{2,0,1:T(8,128)(2,1)S(1)} async-done(((bf16[32,8,128]{2,0,1:T(8,128)(2,1)}), bf16[32,8,128]{2,0,1:T(8,128)(2,1)S(1)}, u32[]{:S(2)}, u32[]{:S(2)}) %all-to-all-start.2) | async-done | bytes 65568 | tf_op jit(solution)/shard_map/all_to_all | solution.py:102
  44.9 4.2 %all-to-all-start = ((bf16[32,8,1024]{2,0,1:T(8,128)(2,1)}), bf16[32,8,1024]{2,0,1:T(8,128)(2,1)S(1)}, u32[]{:S(2)}, u32[]{:S(2)}) async-start(bf16[32,8,1024]{2,0,1:T(8,128)(2,1)} %bitcast.167), calls=%async_computation | async-start | bytes 1048576 | tf_op jit(solution)/shard_map/all_to_all | solution.py:99
  49.7 8.7 %all-to-all-done = bf16[32,8,1024]{2,0,1:T(8,128)(2,1)S(1)} async-done(((bf16[32,8,1024]{2,0,1:T(8,128)(2,1)}), bf16[32,8,1024]{2,0,1:T(8,128)(2,1)S(1)}, u32[]{:S(2)}, u32[]{:S(2)}) %all-to-all-start) | async-done | bytes 524320 | tf_op jit(solution)/shard_map/all_to_all | solution.py:99
  66.7 7.7 %all-reduce = f32[64]{0:T(128)S(1)} all-reduce(f32[64]{0:T(128)S(1)} %dynamic-update-slice), channel_id=2, replica_groups=mesh['seq_0'=16,'seq_1'=4,'head'=8] {'seq_1'}, use_global_device_ids=true, to_apply=%add | all-reduce | flops 64 | bytes 512
  75.1 30.7 %all-gather.6.cloned.1.call-done = f32[4,16,64,128]{3,2,1,0:T(8,128)} async-done(((f32[1,16,64,128]{3,2,1,0:T(8,128)}), f32[4,16,64,128]{3,2,1,0:T(8,128)}) %all-gather.6.cloned.1.call-update) | async-done | bytes 2097168 | tf_op jit(solution)/shard_map/all_gather | solution.py:33
  105.8 2.5 slice_add_fusion.16
  110.0 5.1 %all-to-all-start.4 = ((bf16[32,8,1024]{2,0,1:T(8,128)(2,1)}), bf16[32,8,1024]{2,0,1:T(8,128)(2,1)S(1)}, u32[]{:S(2)}, u32[]{:S(2)}) async-start(bf16[32,8,1024]{2,0,1:T(8,128)(2,1)} %bitcast.166), calls=%async_computation.4 | async-start | bytes 1048576 | tf_op jit(solution)/shard_map/all_to_all | solution.py:100
  117.1 26.5 %all-gather.1 = f32[16,1,16]{2,1,0:T(1,128)S(1)} all-gather(f32[1,1,16]{2,1,0:T(1,128)S(1)} %get-tuple-element.7), channel_id=1, replica_groups=mesh['seq_0'=16,'seq_1'=4,'head'=8] {'seq_0'}, dimensions={0}, use_global_device_ids=true | all-gather | bytes 1088 | tf_op jit(solution)/shard_map/all_gather | solution.py:33
  146.2 1.7 reshape.345
  148.0 1.9 copy.71
  150.9 3.1 convolution_bitcast_fusion.1
  153.9 60.6 %all-gather.8.cloned.1.call-done = f32[16,16,64,128]{3,2,1,0:T(8,128)} async-done(((f32[1,16,64,128]{3,2,1,0:T(8,128)}), f32[16,16,64,128]{3,2,1,0:T(8,128)}) %all-gather.8.cloned.1.call-update) | async-done | bytes 8388624 | tf_op jit(solution)/shard_map/all_gather | solution.py:33
  214.6 4.5 %fusion.60 = (bf16[1,16,64,128]{3,2,1,0:T(8,128)(2,1)S(1)}, f32[1,16,64,128]{3,2,1,0:T(8,128)S(1)}) fusion(pred[]{:T(512)S(6)} %gt.63, pred[]{:T(512)S(6)} %gt.62, f32[4,16,64,128]{3,2,1,0:T(8,128)S(1)} %copy-done.1, f32[16]{0:T(128)S(1)} %get-tuple-element.50, f32[16]{0:T(128)S(1)} %get-tuple-element.49, f32[16]{0:T(128)S(1)} %copy-done.12, pred[]{:T(512)S(6)} %gt.61, ...), kind=kLoop, calls=%fused_computation.164 | loop fusion | flops 7995392 | bytes 11273556 | tf_op jit(solution)/shard_map/convert_element_type | solution.py:155
  219.3 1.6 multiply_reduce_fusion
  220.9 2.2 copy.74
  224.7 1.6 multiply_convert_fusion.2
  226.4 137.5 %all-gather.10.cloned.1.call-done = bf16[1024,4096]{0,1:T(8,128)(2,1)} async-done(((bf16[1024,64]{0,1:T(8,128)(2,1)}), bf16[1024,4096]{0,1:T(8,128)(2,1)}) %all-gather.10.cloned.1.call-update) | async-done | bytes 8388624 | tf_op jit(solution)/shard_map/all_gather | solution.py:172
  363.9 5.7 %convolution_convert_fusion = bf16[256,4096]{1,0:T(8,128)(2,1)S(1)} fusion(bf16[256,1024]{1,0:T(8,128)(2,1)S(1)} %multiply_convert_fusion.2, bf16[1024,4096]{0,1:T(8,128)(2,1)} %all-gather.10.cloned.1.call-done), kind=kOutput, calls=%fused_computation | convolution fusion | flops 2148532224 | bytes 11010048 | tf_op jit(solution)/shard_map/dot_general | solution.py:170
  369.6 38.7 %all_to_all.88 = bf16[8,32,4096]{2,1,0:T(8,128)(2,1)S(1)} all-to-all(bf16[8,32,4096]{2,1,0:T(8,128)(2,1)S(1)} %bitcast.172), channel_id=1, replica_groups=mesh['seq_0'=16,'seq_1'=4,'head'=8] {'head'}, dimensions={0} | all-to-all | bytes 4194304 | tf_op jit(solution)/shard_map/all_to_all | solution.py:51
  (98 shorter events, 27.8 us)
Async XLA Ops:
  6.5 11.6 %copy-start = (bf16[32,1024]{1,0:T(8,128)(2,1)S(1)}, bf16[32,1024]{1,0:T(8,128)(2,1)}, u32[]{:S(2)}) copy-start(bf16[32,1024]{1,0:T(8,128)(2,1)} %param.16) | copy-start | bytes 196612
  6.5 43.1 %copy-start.16 = (f32[16]{0:T(128)S(1)}, f32[16]{0:T(128)}, u32[]{:S(2)}) copy-start(f32[16]{0:T(128)} %param.19) | copy-start | bytes 196
  8.1 18.2 %all-to-all-start.3 = ((bf16[8,2,256]{2,1,0:T(2,128)(2,1)}), bf16[8,2,256]{2,1,0:T(2,128)(2,1)S(1)}, u32[]{:S(2)}, u32[]{:S(2)}) async-start(bf16[8,2,256]{2,1,0:T(2,128)(2,1)} %reshape.437), calls=%async_computation.3 | async-start | bytes 16384 | tf_op jit(solution)/shard_map/all_to_all | solution.py:103
  26.3 9.7 %all-to-all-start.1 = ((bf16[32,8,128]{2,0,1:T(8,128)(2,1)}), bf16[32,8,128]{2,0,1:T(8,128)(2,1)S(1)}, u32[]{:S(2)}, u32[]{:S(2)}) async-start(bf16[32,8,128]{2,0,1:T(8,128)(2,1)} %copy_bitcast_fusion.3), calls=%async_computation.1 | async-start | bytes 131072 | tf_op jit(solution)/shard_map/all_to_all | solution.py:101
  31.3 29.4 %copy-start.14 = (f32[1024]{0:T(1024)S(1)}, f32[1024]{0:T(1024)}, u32[]{:S(2)}) copy-start(f32[1024]{0:T(1024)} %param.23) | copy-start | bytes 12292
  36.0 8.9 %all-to-all-start.2 = ((bf16[32,8,128]{2,0,1:T(8,128)(2,1)}), bf16[32,8,128]{2,0,1:T(8,128)(2,1)S(1)}, u32[]{:S(2)}, u32[]{:S(2)}) async-start(bf16[32,8,128]{2,0,1:T(8,128)(2,1)} %copy_bitcast_fusion.2), calls=%async_computation.2 | async-start | bytes 131072 | tf_op jit(solution)/shard_map/all_to_all | solution.py:102
  44.9 13.6 %all-to-all-start = ((bf16[32,8,1024]{2,0,1:T(8,128)(2,1)}), bf16[32,8,1024]{2,0,1:T(8,128)(2,1)S(1)}, u32[]{:S(2)}, u32[]{:S(2)}) async-start(bf16[32,8,1024]{2,0,1:T(8,128)(2,1)} %bitcast.167), calls=%async_computation | async-start | bytes 1048576 | tf_op jit(solution)/shard_map/all_to_all | solution.py:99
  49.1 56.8 %all-gather.6.cloned.1.call-start = ((), (), s32[]{:S(2)}) async-start(), calls=%async_computation.6 | async-start | bytes 2621440 | tf_op jit(solution)/shard_map/all_gather | solution.py:33
  58.5 2.1 collective-permute-start
  64.4 44.7 %copy-start.7 = (bf16[32,8192]{1,0:T(8,128)(2,1)S(1)}, bf16[32,8192]{1,0:T(8,128)(2,1)}, u32[]{:S(2)}) copy-start(bf16[32,8192]{1,0:T(8,128)(2,1)} %param.15) | copy-start | bytes 1572868
  64.4 150.2 %all-gather.8.cloned.1.call-start = ((), (), s32[]{:S(2)}) async-start(), calls=%async_computation.7 | async-start | bytes 8912896 | tf_op jit(solution)/shard_map/all_gather | solution.py:33
  75.1 34.9 %copy-start.11 = (f32[16]{0:T(128)}, f32[16]{0:T(128)S(1)}, u32[]{:S(2)}) copy-start(f32[16]{0:T(128)S(1)} %get-tuple-element.52) | copy-start | bytes 196
  108.4 255.5 %all-gather.10.cloned.1.call-start = ((), (), s32[]{:S(2)}) async-start(), calls=%async_computation.8 | async-start | bytes 8519680 | tf_op jit(solution)/shard_map/all_gather | solution.py:172
  110.0 34.3 %all-to-all-start.4 = ((bf16[32,8,1024]{2,0,1:T(8,128)(2,1)}), bf16[32,8,1024]{2,0,1:T(8,128)(2,1)S(1)}, u32[]{:S(2)}, u32[]{:S(2)}) async-start(bf16[32,8,1024]{2,0,1:T(8,128)(2,1)} %bitcast.166), calls=%async_computation.4 | async-start | bytes 1048576 | tf_op jit(solution)/shard_map/all_to_all | solution.py:100
  147.9 2.9 copy-start.8
  147.9 2.9 copy-start.9
  147.9 2.9 copy-start.10
  150.6 63.9 %copy-start.1 = (f32[4,16,64,128]{3,2,1,0:T(8,128)S(1)}, f32[4,16,64,128]{3,2,1,0:T(8,128)}, u32[]{:S(2)}) copy-start(f32[4,16,64,128]{3,2,1,0:T(8,128)} %all-gather.6.cloned.1.call-done) | copy-start | bytes 6291460
  150.7 63.9 %copy-start.12 = (f32[16]{0:T(128)S(1)}, f32[16]{0:T(128)}, u32[]{:S(2)}) copy-start(f32[16]{0:T(128)} %copy-done.11) | copy-start | bytes 196
  214.6 4.6 %copy-start.15 = (f32[16]{0:T(128)S(1)}, f32[16]{0:T(128)}, u32[]{:S(2)}) copy-start(f32[16]{0:T(128)} %get-tuple-element.12) | copy-start | bytes 196
  214.6 4.7 %copy-start.5 = (bf16[2,128,16,64]{1,3,2,0:T(8,128)(2,1)S(1)}, bf16[2,128,16,64]{1,3,2,0:T(8,128)(2,1)}, u32[]{:S(2)}) copy-start(bf16[2,128,16,64]{1,3,2,0:T(8,128)(2,1)} %copy-done.4) | copy-start | bytes 1572868
  214.6 4.7 %copy-start.6 = (f32[2,128,16,64]{1,3,2,0:T(8,128)S(1)}, f32[2,128,16,64]{1,3,2,0:T(8,128)}, u32[]{:S(2)}) copy-start(f32[2,128,16,64]{1,3,2,0:T(8,128)} %copy.71) | copy-start | bytes 3145732
  214.6 4.7 %copy-start.17 = (f32[16]{0:T(128)S(1)}, f32[16]{0:T(128)}, u32[]{:S(2)}) copy-start(f32[16]{0:T(128)} %param.21) | copy-start | bytes 196
  214.6 4.7 %copy-start.18 = (f32[2,128,16,64]{1,3,2,0:T(8,128)S(1)}, f32[2,128,16,64]{1,3,2,0:T(8,128)}, u32[]{:S(2)}) copy-start(f32[2,128,16,64]{1,3,2,0:T(8,128)} %convolution_bitcast_fusion.1) | copy-start | bytes 3145732
  (4 other events, 5.4 us)
Sparse Core Ops, SparseCore 0:
  64.5 41.2 all-gather.5
  108.5 106.0 all-gather.7
  217.5 146.3 all-gather.9
where the time goes:
time: 417 us; the launch traced here: 416 us
  waiting for transfers between devices  248 us (59%)
  blocking collectives  72.9 us (17%)
  starting transfers between devices  29.5 us (7%)
  local copies, waits for them, and re-layouts  23.4 us (6%)
  other arithmetic  17.4 us (4%)
  between operations  14.2 us (3%)
  matrix products  10.9 us (3%)
    all_gather x1, waiting for transfers between devices, per_device(): lax.all_gather(out_weight, SEQ, axis=1, tiled=True)  138 us
    all_gather x2, waiting for transfers between devices, entering(): pieces = jax.tree.map(lambda part: lax.all_gather(part, axis), total)  91.4 us
    all_to_all x1, blocking collectives, sent_and_summed(): pieces = lax.all_to_all(split_up(array, dim, count), axis, 0, 0, tiled=True)  38.7 us
    all_gather x1, blocking collectives, entering(): pieces = jax.tree.map(lambda part: lax.all_gather(part, axis), total)  26.5 us
    all_to_all x1, starting transfers between devices, per_device(): lax.all_to_all(dt_raw, 'head', split_axis=1, concat_axis=0, tiled=True)  10 us
    all_to_all x1, waiting for transfers between devices, per_device(): lax.all_to_all(x_proj, 'head', split_axis=1, concat_axis=0, tiled=True)  8.7 us
  transfers between devices with their start and end apart: 9, of which 7 were waited for; matrix products, arithmetic and copies ran while one was open for 9% of the time, Pallas kernels for 0%

commit v1 on v0

--- a/solution.py
+++ b/solution.py
@@ -169,7 +169,9 @@
     normed = (normed.reshape(token_count, -1) * norm_weight).astype(jnp.bfloat16)
     terms = jnp.dot(
         normed,
-        lax.all_gather(out_weight, SEQ, axis=1, tiled=True),
+        jnp.concatenate(
+            lax.all_to_all(jnp.stack([out_weight] * lax.axis_size(SEQ)), SEQ, 0, 0), axis=1
+        ),
         preferred_element_type=jnp.float32,
     )
     mixed = sent_and_summed(terms.astype(jnp.bfloat16), "head", 0)

time: 417 us -> 649 us (1.56)
  blocking collectives: 72.9 us -> 419 us
  waiting for transfers between devices: 248 us -> 132 us
  starting transfers between devices: 29.5 us -> 39.7 us
    unnamed x1, blocking collectives: 7.68 us -> 351 us
    all_gather x1 -> x0, waiting for transfers between devices: 138 us -> none  [per_device(): lax.all_gather(out_weight, SEQ, axis=1, tiled=True)]
    all_gather x2, waiting for transfers between devices: 91.4 us -> 111 us  [entering(): pieces = jax.tree.map(lambda part: lax.all_gather(part, axis), total)]
    all_to_all x0 -> x1, blocking collectives: none -> 12.7 us  [per_device(): lax.all_to_all(z_proj, 'head', split_axis=1, concat_axis=0, tiled=True)]
    all_to_all x1, starting transfers between devices: 5.12 us -> 14.6 us  [per_device(): lax.all_to_all(jnp.stack([out_weight] * lax.axis_size(SEQ)), SEQ, 0, 0)]
    all_to_all x1, blocking collectives: 38.7 us -> 31.1 us  [sent_and_summed(): pieces = lax.all_to_all(split_up(array, dim, count), axis, 0, 0, tiled=True)]
  transfers between devices with their start and end apart: 9 -> 8, of which waited for: 7 -> 7; matrix products, arithmetic and copies ran while one was open for 9% -> 5% of each run, Pallas kernels for 0% -> 0%
where the time goes in v1:
time: 649 us; the launch traced here: 648 us
  blocking collectives  419 us (65%)
  waiting for transfers between devices  132 us (20%)
  starting transfers between devices  39.7 us (6%)
  local copies, waits for them, and re-layouts  20.2 us (3%)
  between operations  14.6 us (2%)
  other arithmetic  12.6 us (2%)
  matrix products  10.2 us (2%)
    unnamed x1, blocking collectives  351 us
    all_gather x2, waiting for transfers between devices, entering(): pieces = jax.tree.map(lambda part: lax.all_gather(part, axis), total)  111 us
    all_to_all x1, blocking collectives, sent_and_summed(): pieces = lax.all_to_all(split_up(array, dim, count), axis, 0, 0, tiled=True)  31.1 us
    all_gather x1, blocking collectives, entering(): pieces = jax.tree.map(lambda part: lax.all_gather(part, axis), total)  24.1 us
    all_to_all x1, starting transfers between devices, per_device(): lax.all_to_all(jnp.stack([out_weight] * lax.axis_size(SEQ)), SEQ, 0, 0)  14.6 us
  transfers between devices with their start and end apart: 8, of which 7 were waited for; matrix products, arithmetic and copies ran while one was open for 5% of the time, Pallas kernels for 0%

profile of v1, /device:TPU:1, one launch (start us, length us, event | category | flops | bytes accessed | tf_op | source)
XLA Modules:
  0.0 647.8 jit_solution(13853131028433914085)
XLA Ops:
  8.1 10.1 %all-to-all-start.3 = ((bf16[8,2,256]{2,1,0:T(2,128)(2,1)}), bf16[8,2,256]{2,1,0:T(2,128)(2,1)S(1)}, u32[]{:S(2)}, u32[]{:S(2)}) async-start(bf16[8,2,256]{2,1,0:T(2,128)(2,1)} %reshape.535), calls=%async_computation.3 | async-start | bytes 16384 | tf_op jit(solution)/shard_map/all_to_all | solution.py:103
  18.8 4.0 all-to-all-done.3
  22.8 4.0 all-to-all-start.1
  28.3 3.4 all-to-all-done.1
  31.6 4.0 all-to-all-start.2
  35.7 1.9 copy.92
  37.6 3.0 all-to-all-done.2
  40.5 4.2 all-to-all-start
  44.8 9.3 %all-to-all-done = bf16[32,8,1024]{2,0,1:T(8,128)(2,1)S(1)} async-done(((bf16[32,8,1024]{2,0,1:T(8,128)(2,1)}), bf16[32,8,1024]{2,0,1:T(8,128)(2,1)S(1)}, u32[]{:S(2)}, u32[]{:S(2)}) %all-to-all-start) | async-done | bytes 524320 | tf_op jit(solution)/shard_map/all_to_all | solution.py:99
  54.1 12.7 %all_to_all.93 = bf16[32,8,1024]{2,0,1:T(8,128)(2,1)S(1)} all-to-all(bf16[32,8,1024]{2,0,1:T(8,128)(2,1)S(1)} %bitcast.164), channel_id=1, replica_groups=mesh['seq_0'=16,'seq_1'=4,'head'=8] {'head'}, dimensions={1} | all-to-all | bytes 1048576 | tf_op jit(solution)/shard_map/all_to_all | solution.py:100
  66.8 4.3 stack.5
  71.1 14.6 %all-to-all-start.5 = ((bf16[64,1024,64]{1,2,0:T(8,128)(2,1)}), bf16[64,1024,64]{1,2,0:T(8,128)(2,1)}, u32[]{:S(2)}, u32[]{:S(2)}) async-start(bf16[64,1024,64]{1,2,0:T(8,128)(2,1)} %stack.5), calls=%async_computation.5 | async-start | bytes 16777216 | tf_op jit(solution)/shard_map/all_to_all | solution.py:173
  86.6 2.8 collective-permute-start
  96.4 351.0 %all-reduce = f32[64]{0:T(128)S(1)} all-reduce(f32[64]{0:T(128)S(1)} %dynamic-update-slice), channel_id=2, replica_groups=mesh['seq_0'=16,'seq_1'=4,'head'=8] {'seq_1'}, use_global_device_ids=true, to_apply=%add | all-reduce | flops 64 | bytes 512
  447.6 39.3 %all-gather.5.cloned.1.call-done = f32[4,16,64,128]{3,2,1,0:T(8,128)} async-done(((f32[1,16,64,128]{3,2,1,0:T(8,128)}), f32[4,16,64,128]{3,2,1,0:T(8,128)}) %all-gather.5.cloned.1.call-update) | async-done | bytes 2097168 | tf_op jit(solution)/shard_map/all_gather | solution.py:33
  486.9 2.5 slice_add_fusion.16
  489.7 24.1 %all-gather.1 = f32[16,1,16]{2,1,0:T(1,128)S(1)} all-gather(f32[1,1,16]{2,1,0:T(1,128)S(1)} %get-tuple-element.7), channel_id=1, replica_groups=mesh['seq_0'=16,'seq_1'=4,'head'=8] {'seq_0'}, dimensions={0}, use_global_device_ids=true | all-gather | bytes 1088 | tf_op jit(solution)/shard_map/all_gather | solution.py:33
  516.9 1.7 reshape.444
  518.6 1.9 copy.77
  520.8 3.1 convolution_bitcast_fusion.1
  523.9 71.7 %all-gather.7.cloned.1.call-done = f32[16,16,64,128]{3,2,1,0:T(8,128)} async-done(((f32[1,16,64,128]{3,2,1,0:T(8,128)}), f32[16,16,64,128]{3,2,1,0:T(8,128)}) %all-gather.7.cloned.1.call-update) | async-done | bytes 8388624 | tf_op jit(solution)/shard_map/all_gather | solution.py:33
  595.7 4.5 fusion.59
  602.7 6.0 convolution_convert_fusion
  608.8 31.1 %all_to_all.94 = bf16[8,32,4096]{2,1,0:T(8,128)(2,1)S(1)} all-to-all(bf16[8,32,4096]{2,1,0:T(8,128)(2,1)S(1)} %bitcast.163), channel_id=1, replica_groups=mesh['seq_0'=16,'seq_1'=4,'head'=8] {'head'}, dimensions={0} | all-to-all | bytes 4194304 | tf_op jit(solution)/shard_map/all_to_all | solution.py:51
  (109 shorter events, 18.0 us)
Async XLA Ops:
  6.5 38.2 %copy-start.6 = (bf16[32,8192]{1,0:T(8,128)(2,1)S(1)}, bf16[32,8192]{1,0:T(8,128)(2,1)}, u32[]{:S(2)}) copy-start(bf16[32,8192]{1,0:T(8,128)(2,1)} %param.15) | copy-start | bytes 1572868
  8.1 14.7 %all-to-all-start.3 = ((bf16[8,2,256]{2,1,0:T(2,128)(2,1)}), bf16[8,2,256]{2,1,0:T(2,128)(2,1)S(1)}, u32[]{:S(2)}, u32[]{:S(2)}) async-start(bf16[8,2,256]{2,1,0:T(2,128)(2,1)} %reshape.535), calls=%async_computation.3 | async-start | bytes 16384 | tf_op jit(solution)/shard_map/all_to_all | solution.py:103
  22.8 8.8 %all-to-all-start.1 = ((bf16[32,8,128]{2,0,1:T(8,128)(2,1)}), bf16[32,8,128]{2,0,1:T(8,128)(2,1)S(1)}, u32[]{:S(2)}, u32[]{:S(2)}) async-start(bf16[32,8,128]{2,0,1:T(8,128)(2,1)} %copy_bitcast_fusion.3), calls=%async_computation.1 | async-start | bytes 131072 | tf_op jit(solution)/shard_map/all_to_all | solution.py:101
  31.6 8.9 %all-to-all-start.2 = ((bf16[32,8,128]{2,0,1:T(8,128)(2,1)}), bf16[32,8,128]{2,0,1:T(8,128)(2,1)S(1)}, u32[]{:S(2)}, u32[]{:S(2)}) async-start(bf16[32,8,128]{2,0,1:T(8,128)(2,1)} %copy_bitcast_fusion.2), calls=%async_computation.2 | async-start | bytes 131072 | tf_op jit(solution)/shard_map/all_to_all | solution.py:102
  35.7 31.1 %copy-start.7 = (bf16[1024,64]{0,1:T(8,128)(2,1)S(1)}, bf16[1024,64]{0,1:T(8,128)(2,1)}, u32[]{:S(2)}) copy-start(bf16[1024,64]{0,1:T(8,128)(2,1)} %param.27) | copy-start | bytes 393220
  40.5 13.6 %all-to-all-start = ((bf16[32,8,1024]{2,0,1:T(8,128)(2,1)}), bf16[32,8,1024]{2,0,1:T(8,128)(2,1)S(1)}, u32[]{:S(2)}, u32[]{:S(2)}) async-start(bf16[32,8,1024]{2,0,1:T(8,128)(2,1)} %bitcast.157), calls=%async_computation | async-start | bytes 1048576 | tf_op jit(solution)/shard_map/all_to_all | solution.py:99
  71.1 14.6 %copy-start.22 = (f32[16]{0:T(128)S(1)}, f32[16]{0:T(128)}, u32[]{:S(2)}) copy-start(f32[16]{0:T(128)} %param.20) | copy-start | bytes 196
  71.1 14.7 %copy-start.20 = (f32[2,128]{1,0:T(2,128)S(1)}, f32[2,128]{1,0:T(2,128)}, u32[]{:S(2)}) copy-start(f32[2,128]{1,0:T(2,128)} %param.25) | copy-start | bytes 3076
  71.1 14.7 %copy-start.9 = (f32[4,2,128]{2,1,0:T(2,128)S(1)}, f32[4,2,128]{2,1,0:T(2,128)}, u32[]{:S(2)}) copy-start(f32[4,2,128]{2,1,0:T(2,128)} %param.24) | copy-start | bytes 12292
  71.1 14.7 %copy-start.8 = (f32[4,1024]{1,0:T(4,128)S(1)}, f32[4,1024]{1,0:T(4,128)}, u32[]{:S(2)}) copy-start(f32[4,1024]{1,0:T(4,128)} %param.22) | copy-start | bytes 49156
  71.1 14.9 %copy-start.11 = (f32[16]{0:T(128)S(1)}, f32[16]{0:T(128)}, u32[]{:S(2)}) copy-start(f32[16]{0:T(128)} %param.19) | copy-start | bytes 196
  71.1 531.6 %all-to-all-start.5 = ((bf16[64,1024,64]{1,2,0:T(8,128)(2,1)}), bf16[64,1024,64]{1,2,0:T(8,128)(2,1)}, u32[]{:S(2)}, u32[]{:S(2)}) async-start(bf16[64,1024,64]{1,2,0:T(8,128)(2,1)} %stack.5), calls=%async_computation.5 | async-start | bytes 16777216 | tf_op jit(solution)/shard_map/all_to_all | solution.py:173
  85.7 401.2 %all-gather.5.cloned.1.call-start = ((), (), s32[]{:S(2)}) async-start(), calls=%async_computation.7 | async-start | bytes 2621440 | tf_op jit(solution)/shard_map/all_gather | solution.py:33
  86.6 3.8 collective-permute-start
  94.2 501.4 %all-gather.7.cloned.1.call-start = ((), (), s32[]{:S(2)}) async-start(), calls=%async_computation.8 | async-start | bytes 8912896 | tf_op jit(solution)/shard_map/all_gather | solution.py:33
  520.6 75.0 %copy-start.1 = (f32[4,16,64,128]{3,2,1,0:T(8,128)S(1)}, f32[4,16,64,128]{3,2,1,0:T(8,128)}, u32[]{:S(2)}) copy-start(f32[4,16,64,128]{3,2,1,0:T(8,128)} %all-gather.5.cloned.1.call-done) | copy-start | bytes 6291460
  520.6 75.0 %copy-start.12 = (f32[16]{0:T(128)S(1)}, f32[16]{0:T(128)}, u32[]{:S(2)}) copy-start(f32[16]{0:T(128)} %get-tuple-element.32) | copy-start | bytes 196
  520.6 75.0 %copy-start.13 = (f32[16]{0:T(128)S(1)}, f32[16]{0:T(128)}, u32[]{:S(2)}) copy-start(f32[16]{0:T(128)} %get-tuple-element.33) | copy-start | bytes 196
  520.6 75.0 %copy-start.14 = (f32[16]{0:T(128)S(1)}, f32[16]{0:T(128)}, u32[]{:S(2)}) copy-start(f32[16]{0:T(128)} %get-tuple-element.34) | copy-start | bytes 196
  520.6 75.0 %copy-start.15 = (f32[16]{0:T(128)S(1)}, f32[16]{0:T(128)}, u32[]{:S(2)}) copy-start(f32[16]{0:T(128)} %get-tuple-element.35) | copy-start | bytes 196
  520.6 75.0 %copy-start.16 = (f32[16]{0:T(128)S(1)}, f32[16]{0:T(128)}, u32[]{:S(2)}) copy-start(f32[16]{0:T(128)} %get-tuple-element.36) | copy-start | bytes 196
  520.6 75.0 %copy-start.17 = (f32[16]{0:T(128)S(1)}, f32[16]{0:T(128)}, u32[]{:S(2)}) copy-start(f32[16]{0:T(128)} %get-tuple-element.37) | copy-start | bytes 196
  520.6 75.0 %copy-start.18 = (f32[16]{0:T(128)S(1)}, f32[16]{0:T(128)}, u32[]{:S(2)}) copy-start(f32[16]{0:T(128)} %get-tuple-element.38) | copy-start | bytes 196
  520.7 75.0 %copy-start.19 = (f32[16]{0:T(128)S(1)}, f32[16]{0:T(128)}, u32[]{:S(2)}) copy-start(f32[16]{0:T(128)} %get-tuple-element.39) | copy-start | bytes 196
  (9 other events, 40.0 us)
Sparse Core Ops, SparseCore 0:
  94.3 392.5 all-gather.4
  489.6 105.9 all-gather.6
